TPU v7x, 512 devices: a whole 4x4x16 slice. The times are simulated.
512 devices in a mesh: nodes: 128 (over z_hi, y, x, core), heads: 4 (over z_lo).
Axes of the slice: x: 4, y: 4, z: 16 (z_hi: 4, z_lo: 4; z = z_hi * 4 + z_lo), core: 2. Of those that a mesh axis runs over, the one named last changes fastest.
Arguments:
- grid_state: bfloat16 [131072, 1024], P('nodes', 'heads'), may hold values from -6 to 6
- mesh_state: bfloat16 [32768, 1024], P('nodes', 'heads'), may hold values from -6 to 6
- encoder_query: bfloat16 [1024, 512], P('nodes', 'heads'), may hold values from -0.1875 to 0.1875
- encoder_key: bfloat16 [1024, 512], P('nodes', 'heads'), may hold values from -0.1875 to 0.1875
- encoder_value: bfloat16 [1024, 512], P('nodes', 'heads'), may hold values from -0.1875 to 0.1875
- encoder_output: bfloat16 [512, 1024], P('heads', 'nodes'), may hold values from -0.25 to 0.25
- window_query: bfloat16 [1024, 512], P('nodes', 'heads'), may hold values from -0.1875 to 0.1875
- window_key: bfloat16 [1024, 512], P('nodes', 'heads'), may hold values from -0.1875 to 0.1875
- window_value: bfloat16 [1024, 512], P('nodes', 'heads'), may hold values from -0.1875 to 0.1875
- window_output: bfloat16 [512, 1024], P('heads', 'nodes'), may hold values from -0.25 to 0.25
- expand_weight: bfloat16 [1024, 2048], P('nodes', 'heads'), may hold values from -0.1875 to 0.1875
- shrink_weight: bfloat16 [2048, 1024], P('heads', 'nodes'), may hold values from -0.125 to 0.125
- decoder_query: bfloat16 [1024, 512], P('nodes', 'heads'), may hold values from -0.1875 to 0.1875
- decoder_key: bfloat16 [1024, 512], P('nodes', 'heads'), may hold values from -0.1875 to 0.1875
- decoder_value: bfloat16 [1024, 512], P('nodes', 'heads'), may hold values from -0.1875 to 0.1875
- decoder_output: bfloat16 [512, 1024], P('heads', 'nodes'), may hold values from -0.25 to 0.25
- encoder_blocks: int32 [256, 8], P('nodes'), may hold values from 0 to 1023, as said below
- encoder_count: int32 [256], P('nodes'), may hold values from 2 to 8, as said below
- window_offsets: int32 [256, 4], P('nodes'), may hold values from -2 to 2, as said below
- decoder_blocks: int32 [1024, 3], P('nodes'), may hold values from 0 to 255, as said below
- decoder_count: int32 [1024], P('nodes'), may hold values from 1 to 3, as said below
Outputs:
- grid_out: bfloat16 [131072, 1024], P('nodes', 'heads')
- mesh_out: bfloat16 [32768, 1024], P('nodes', 'heads')
Inputs may be any that keep to these rules, and one draw needn't show every extreme that they name: `encoder_blocks`: row m names 8 different grid blocks; each lies among the grid blocks of the index of nodes that holds mesh block m, or in the nearer half of the grid blocks of the index on either side. The first encoder_count[m] slots of row m are live; every mesh block held by the first or last eighth of the indices of nodes has all 8 slots live. `window_offsets`: each row holds 4 different offsets, the first of them 0. `decoder_blocks`: row g names 3 different mesh blocks; each lies among the mesh blocks of the index of nodes that holds grid block g, or is the one block next to them on either side. The first decoder_count[g] slots of row g are live; every grid block of the first index of nodes has all 3 slots live.
All inputs are finite; a program needn't handle non-finite values.
Results may differ from a plain program's by a relative error of at most 0.012.
Values may be sent and summed in bfloat16 or wider, within the bound.
No kernel may reach another device: no remote copies, remote signals or barrier semaphores. Data moves between devices by JAX's collectives and lax.ppermute only.
A program may use at most 64 MiB of HBM per device.

v0:
```python
import functools

import jax
import jax.numpy as jnp
from jax import lax
from jax.experimental import pallas as pl
from jax.experimental.pallas import tpu as pltpu
from jax.sharding import Mesh
from jax.sharding import PartitionSpec as P


HEAD_DIM = 64
TILE = 128
PAIR = 2 * HEAD_DIM
D = 1024
SCALE = HEAD_DIM ** (-0.5)
EPSILON = 1e-05
NODES = ("zh", "y", "x", "core")
F32 = jnp.float32
BF16 = jnp.bfloat16


def in_vmem():
    return pl.BlockSpec(memory_space=pltpu.VMEM)


def in_smem():
    return pl.BlockSpec(memory_space=pltpu.SMEM)


def in_any():
    return pl.BlockSpec(memory_space=pltpu.HBM)


def call(kernel, outs, specs, scratch=(), flops=1 << 28, room=12):
    return pl.pallas_call(
        kernel,
        out_shape=tuple(jax.ShapeDtypeStruct(shape, BF16) for shape in outs),
        in_specs=list(specs),
        out_specs=tuple(in_vmem() for _ in outs),
        scratch_shapes=list(scratch),
        compiler_params=pltpu.CompilerParams(vmem_limit_bytes=room << 20),
        cost_estimate=pl.CostEstimate(flops=flops, bytes_accessed=1 << 20, transcendentals=0),
    )


def mm(a, b):
    return jnp.dot(a, b, preferred_element_type=F32)


def mm_t(a, b):
    return lax.dot_general(a, b, (((1,), (1,)), ((), ())), preferred_element_type=F32)


def normalize(values):
    values = values.astype(F32)
    average = jnp.mean(values, axis=-1, keepdims=True)
    centred = values - average
    spread = jnp.mean(centred * centred, axis=-1, keepdims=True)
    return (centred * lax.rsqrt(spread + EPSILON)).astype(BF16)


def wide(ref):
    return jnp.concatenate([ref[k] for k in range(ref.shape[0])], axis=-1)


def pack_kernel(*refs):
    *sources, out = refs
    t = 0
    for source in sources:
        whole = source[...]
        for k in range(0, whole.shape[1], 128):
            for g in range(out.shape[0]):
                out[g, t] = whole[:, k : k + 128]
            t += 1


def regroup_kernel(counts, src, near, far):
    first = 0
    for out, members in zip((near, far), counts):
        column = 0
        for count in members:
            for h in range(4):
                for k in range(count):
                    for z in range(4):
                        tile = src[z * 4 + h, first + k]
                        if out is near:
                            for g in range(near.shape[0]):
                                near[g, z, :, column : column + 128] = tile
                        else:
                            far[z, :, column : column + 128] = tile
                    column += 128
            first += count


def own_kernel(pos, grid, mesh, out):
    rows = grid.shape[1]
    out[:rows, :] = grid[pos[2]]
    out[rows:, :] = mesh[pos[2]]


class Chunk:
    def __init__(self, widths):
        self.starts, self.widths, at = [], widths, 0
        for width in widths:
            self.starts.append(at)
            at += width

    def copies(self, k, dst, mine, theirs, core, sems):
        start, width = self.starts[k], self.widths[k]
        made = []
        for z in range(4):
            for n, (src, half) in enumerate(((mine, core), (theirs, 1 - core))):
                made.append(
                    pltpu.make_async_copy(
                        src.at[:, z, :, pl.ds(start, width)],
                        dst.at[z, :, half],
                        sems.at[z * 2 + n],
                    )
                )
        return made


CHUNK_A = Chunk((512, 512, 512))
CHUNK_B = Chunk((512,) * 5 + (2048,) * 2 + (512,) * 4)


def weight_scratch(chunk, members):
    return [pltpu.VMEM((4, 16, 2, 8, chunk.widths[m]), BF16) for m in members] + [
        pltpu.SemaphoreType.DMA((len(members), 8))
    ]


class Weights:
    def __init__(self, chunk, members, pos, mine, theirs, buffers, sems):
        core = pos[1]
        self.buffers = buffers
        self.made = [
            chunk.copies(m, buffers[n], mine, theirs, core, sems.at[n])
            for n, m in enumerate(members)
        ]
        for group in self.made:
            for copy in group:
                copy.start()

    def get(self, n):
        for copy in self.made[n]:
            copy.wait()
        buffer = self.buffers[n]
        return buffer.reshape(D, buffer.shape[-1])[...]


def softmax_mix(queries, keys, values, dead):
    scores = jnp.where(dead, -1e30, mm_t(queries, keys))
    weights = jnp.exp(scores - jnp.max(scores, axis=-1, keepdims=True))
    weights = weights * (1.0 / jnp.sum(weights, axis=-1, keepdims=True))
    return mm(weights.astype(BF16), values)


def two_heads(queries, keys, values, dead):
    first = lax.broadcasted_iota(jnp.int32, queries.shape, 1) < HEAD_DIM
    zero = jnp.zeros_like(queries)
    stacked = jnp.concatenate(
        [jnp.where(first, queries, zero), jnp.where(first, zero, queries)], axis=0
    )
    mixed = softmax_mix(stacked, keys, values, dead)
    rows = queries.shape[0]
    return jnp.where(first, mixed[:rows], mixed[rows:]).astype(BF16)


def inputs_kernel(
    pos, x0, x1, x2, x3, mine, theirs, staged, grid, mesh, wk, wv, wq, sems
):
    weights = Weights(CHUNK_A, (0, 1, 2), pos, mine, theirs, (wk, wv, wq), sems)
    head = pos[2]
    rows, half = grid.shape[1], mesh.shape[1] // 2
    for k, part in enumerate((x0, x1, x2, x3)):
        grid[head ^ k] = part[:rows, :]
        mesh[head ^ k] = part[rows:, :]
    grid_norm = normalize(wide(grid))
    mesh_norm = normalize(wide(mesh))
    keys = mm(grid_norm, weights.get(0)).astype(BF16)
    for j in range(4):
        staged[j, :rows, :PAIR] = keys[:, j * PAIR : (j + 1) * PAIR]
    values = mm(grid_norm, weights.get(1)).astype(BF16)
    for j in range(4):
        staged[j, :rows, PAIR:] = values[:, j * PAIR : (j + 1) * PAIR]
    queries = (mm(mesh_norm, weights.get(2)) * SCALE).astype(BF16)
    for j in range(4):
        staged[j, rows:, :PAIR] = queries[:half, j * PAIR : (j + 1) * PAIR]
        staged[j, rows:, PAIR:] = queries[half:, j * PAIR : (j + 1) * PAIR]


def encode_kernel(pos, blocks, count, own, before, after, out, tiles, picked):
    rows = own.shape[1] - 32
    for j in range(2):
        for k in range(2):
            part = slice(k * TILE, (k + 1) * TILE)
            tiles[j * 2 + k] = before[j, part]
            tiles[12 + j * 2 + k] = after[j, part]
    for j in range(4):
        for k in range(rows // TILE):
            tiles[4 + j * 2 + k] = own[j, k * TILE : (k + 1) * TILE]
    start = pos[0] * 8 - 4
    slots = blocks.shape[1]
    column = lax.broadcasted_iota(jnp.int32, (2 * TILE, slots * TILE), 1)
    for m in range(2):
        for s in range(slots):
            index = jnp.clip(blocks[m, s] - start, 0, 15)
            picked[s * TILE : (s + 1) * TILE, :] = tiles[index]
        queries = jnp.concatenate(
            [
                own[2 * m + g, rows:, side * PAIR : (side + 1) * PAIR]
                for g in range(2)
                for side in range(2)
            ],
            axis=0,
        )
        mixed = two_heads(queries, picked[:, :PAIR], picked[:, PAIR:], column >= count[m] * TILE)
        out[2 * m] = mixed[:64]
        out[2 * m + 1] = mixed[64:]


def first_kernel(pos, encoded, mesh, mine, theirs, qkv, kept, wo, wq, wk, wv, sems):
    weights = Weights(CHUNK_B, (0, 1, 2, 3), pos, mine, theirs, (wo, wq, wk, wv), sems)
    update = mm_t(wide(encoded), weights.get(0))
    mesh_one = (wide(mesh).astype(F32) + update).astype(BF16)
    kept[...] = mesh_one
    norm_one = normalize(mesh_one)
    for n, scaling in enumerate((SCALE, 1.0, 1.0)):
        part = (mm(norm_one, weights.get(1 + n)) * scaling).astype(BF16)
        for j in range(4):
            qkv[j, :, n * PAIR : (n + 1) * PAIR] = part[:, j * PAIR : (j + 1) * PAIR]


def window_kernel(pos, offsets, own, before, after, out, tiles, picked):
    for j in range(4):
        half = slice((j % 2) * 64, (j % 2) * 64 + 64)
        tiles[j // 2, half] = before[j]
        tiles[2 + j // 2, half] = own[j, :, PAIR:]
        tiles[4 + j // 2, half] = after[j]
    slots = offsets.shape[1]
    slot = lax.broadcasted_iota(jnp.int32, (2 * TILE, slots * TILE), 1) // TILE
    for m in range(2):
        alive = jnp.zeros((2 * TILE, slots * TILE), jnp.int32)
        for s in range(slots):
            offset = offsets[m, s]
            picked[s * TILE : (s + 1) * TILE, :] = tiles[jnp.clip(m + 2 + offset, 0, 5)]
            reached = pos[0] * 2 + m + offset
            live = jnp.where((reached >= 0) & (reached < pos[3]), 1, 0)
            alive = jnp.where(slot == s, live, alive)
        queries = jnp.concatenate([own[2 * m, :, :PAIR], own[2 * m + 1, :, :PAIR]], axis=0)
        mixed = two_heads(queries, picked[:, :PAIR], picked[:, PAIR:], alive == 0)
        out[2 * m] = mixed[:64]
        out[2 * m + 1] = mixed[64:]


def second_kernel(
    pos, windowed, kept, mine, theirs, mesh_out, kv, wo, up, down, wk, wv, sems
):
    weights = Weights(CHUNK_B, (4, 5, 6, 7, 8), pos, mine, theirs, (wo, up, down, wk, wv), sems)
    update = mm_t(wide(windowed), weights.get(0))
    mesh_two = (kept[...].astype(F32) + update).astype(BF16)
    hidden = mm(normalize(mesh_two), weights.get(1))
    hidden = (0.5 * hidden * (1.0 + lax.erf(hidden * (2.0**-0.5)))).astype(BF16)
    result = (mesh_two.astype(F32) + mm_t(hidden, weights.get(2))).astype(BF16)
    for j in range(4):
        mesh_out[j] = result[:, j * 256 : (j + 1) * 256]
    norm_three = normalize(result)
    keys = mm(norm_three, weights.get(3)).astype(BF16)
    values = mm(norm_three, weights.get(4)).astype(BF16)
    kv[:, :512] = keys
    kv[:, 512:] = values


def queries_kernel(pos, grid, mine, theirs, out, wq, sems):
    weights = Weights(CHUNK_B, (9,), pos, mine, theirs, (wq,), sems)
    out[...] = (mm(normalize(wide(grid)), weights.get(0)) * SCALE).astype(BF16)


def decode_kernel(pos, blocks, count, grid, queries, own, before, after, mine, theirs, out, wo,
                  tiles, picked, sems):
    weights = Weights(CHUNK_B, (10,), pos, mine, theirs, (wo,), sems)
    tiles[0] = before[...]
    for j in range(4):
        half = slice((j % 2) * 64, (j % 2) * 64 + 64)
        tiles[1 + j // 2, half] = own[j]
    tiles[3] = after[...]
    start = pos[0] * 2 - 1
    slots = blocks.shape[1]
    column = lax.broadcasted_iota(jnp.int32, (2 * TILE, slots * TILE), 1)
    mixtures = []
    for t in range(2):
        row = pos[2] * 2 + t
        for s in range(slots):
            index = jnp.clip(blocks[row, s] - start, 0, 3)
            picked[s * TILE : (s + 1) * TILE, :] = tiles[index]
        dead = column >= count[row] * TILE
        mixtures.append(
            jnp.concatenate(
                [
                    two_heads(
                        queries[t * TILE : (t + 1) * TILE, j * PAIR : (j + 1) * PAIR],
                        picked[:, j * PAIR : (j + 1) * PAIR],
                        picked[:, 512 + j * PAIR : 512 + (j + 1) * PAIR],
                        dead,
                    )
                    for j in range(4)
                ],
                axis=1,
            )
        )
    decoded = jnp.concatenate(mixtures, axis=0)
    result = (wide(grid).astype(F32) + mm_t(decoded, weights.get(0))).astype(BF16)
    for j in range(4):
        out[j] = result[:, j * 256 : (j + 1) * 256]


def exchange(x):
    return lax.all_to_all(x, "heads", 0, 0, tiled=True)


def halo(last, first):
    size = lax.axis_size(NODES)
    up = [(i, i + 1) for i in range(size - 1)]
    down = [(j, i) for i, j in up]
    return lax.ppermute(last, NODES, up), lax.ppermute(first, NODES, down)


def after_it(x, other):
    return lax.optimization_barrier((x, other))[0]


def in_hbm(x):
    return pltpu.with_memory_space_constraint(x, pltpu.HBM)


def over_cores(x):
    return lax.ppermute(x, "core", [(0, 1), (1, 0)])


def trade(parts):
    out = [parts[0]]
    for k in range(1, 4):
        out.append(lax.ppermute(parts[k], "heads", [(i, i ^ k) for i in range(4)]))
    return out


def pack(sources):
    (tiles,) = call(
        pack_kernel, [(16, 20, 8, 128)], [in_vmem()] * len(sources), room=56
    )(*sources)
    return tiles


def over_plane(x):
    return lax.all_to_all(x, ("y", "x"), 0, 0, tiled=True)


def local(
    grid_state,
    mesh_state,
    encoder_query,
    encoder_key,
    encoder_value,
    encoder_output,
    window_query,
    window_key,
    window_value,
    window_output,
    expand_weight,
    shrink_weight,
    decoder_query,
    decoder_key,
    decoder_value,
    decoder_output,
    encoder_blocks,
    encoder_count,
    window_offsets,
    decoder_blocks,
    decoder_count,
):
    position = lax.axis_index(NODES)
    mesh_tiles = lax.axis_size(NODES) * 2
    pos = jnp.stack(
        [position, lax.axis_index("core"), lax.axis_index("heads"), jnp.int32(mesh_tiles),
         lax.axis_index("zh")]
    ).astype(jnp.int32)

    counts = ((1, 1, 1), (1, 1, 1, 1, 1, 4, 4, 1, 1, 1, 1))
    tiles = pack(
        (
            encoder_key, encoder_value, encoder_query, encoder_output.T, window_query, window_key,
            window_value, window_output.T, expand_weight, shrink_weight.T, decoder_key,
            decoder_value, decoder_query, decoder_output.T,
        )
    )
    tiles = lax.all_to_all(tiles, ("zh", "heads"), 0, 0, tiled=True)
    copies_a, rows = call(
        functools.partial(regroup_kernel, counts),
        [(16, 4, 8, 1536), (4, 8, 8704)],
        [in_vmem()],
    )(tiles)
    mine = lax.all_gather(rows, ("y", "x"))
    mine_a = over_plane(copies_a)
    theirs_a = over_cores(mine_a)


    head = lax.axis_index("heads")
    grid_parts, mesh_parts = grid_state.reshape(4, 256, 256), mesh_state.reshape(4, 64, 256)
    both = call(
        own_kernel, [(320, 256)], [in_smem(), in_vmem(), in_vmem()], room=8
    )(pos, grid_parts, mesh_parts)
    both += tuple(
        jnp.concatenate(
            [
                lax.dynamic_index_in_dim(after_it(x, copies_a), head ^ k, 0, False)
                for x in (grid_parts, mesh_parts)
            ]
        )
        for k in range(1, 4)
    )
    sent, grid, mesh = call(
        inputs_kernel,
        [(4, 288, 256), (4, 256, 256), (4, 64, 256)],
        [in_smem()] + [in_vmem()] * 4 + [in_any(), in_any()],
        weight_scratch(CHUNK_A, (0, 1, 2)),
        room=16,
    )(pos, *trade(both), mine_a, theirs_a)
    own = exchange(sent)
    before, after = halo(own[2:, :256], own[:2, :256])
    (sent,) = call(
        encode_kernel,
        [(4, 64, 128)],
        [in_smem()] * 3 + [in_vmem()] * 3,
        [pltpu.VMEM((16, TILE, 256), BF16), pltpu.VMEM((8 * TILE, 256), BF16)],
    )(pos, encoder_blocks, encoder_count, own, before, after)
    encoded = exchange(sent)
    mine = after_it(mine, sent)
    theirs_b = over_cores(mine[:, :, :, :2048])
    theirs = over_cores(mine)
    mine, late = in_hbm(mine), in_hbm(theirs)
    sent, kept = call(
        first_kernel,
        [(4, 64, 384), (64, D)],
        [in_smem(), in_vmem(), in_vmem(), in_any(), in_any()],
        weight_scratch(CHUNK_B, (0, 1, 2, 3)),
        room=16,
    )(pos, encoded, mesh, mine, theirs_b)
    own = exchange(sent)
    side = own[:, :, PAIR:]
    before, after = halo(side, side)
    (sent,) = call(
        window_kernel,
        [(4, 64, 128)],
        [in_smem()] * 2 + [in_vmem()] * 3,
        [pltpu.VMEM((6, TILE, 256), BF16), pltpu.VMEM((4 * TILE, 256), BF16)],
    )(pos, window_offsets, own, before, after)
    windowed = exchange(sent)
    sent, spread = call(
        second_kernel,
        [(4, 64, 256), (64, D)],
        [in_smem(), in_vmem(), in_vmem()] + [in_any()] * 2,
        weight_scratch(CHUNK_B, (4, 5, 6, 7, 8)),
        room=24,
    )(pos, windowed, kept, mine, theirs)
    own = lax.all_gather(spread, "heads")
    before, after = halo(own[2:].reshape(TILE, D), own[:2].reshape(TILE, D))
    mesh_out = exchange(sent).reshape(256, 256)
    (queries,) = call(
        queries_kernel,
        [(256, 512)],
        [in_smem(), in_vmem()] + [in_any()] * 2,
        weight_scratch(CHUNK_B, (9,)),
        room=12,
    )(pos, grid, mine, late)
    last = weight_scratch(CHUNK_B, (10,))
    (sent,) = call(
        decode_kernel,
        [(4, 256, 256)],
        [in_smem()] * 3 + [in_vmem()] * 5 + [in_any()] * 2,
        last[:-1]
        + [pltpu.VMEM((4, TILE, D), BF16), pltpu.VMEM((3 * TILE, D), BF16), last[-1]],
        room=16,
    )(pos, decoder_blocks, decoder_count, grid, queries, own, before, after, mine, late)
    grid_out = exchange(sent).reshape(1024, 256)
    return grid_out, mesh_out


def solution(mesh):
    sizes = (4, 4, 4, 2)
    fine = Mesh(mesh.devices.reshape(*sizes, mesh.devices.shape[1]), (*NODES, "heads"))
    both, flipped = P(NODES, "heads"), P("heads", NODES)
    in_specs = (
        both, both, both, both, both, flipped, both, both, both, flipped, both, flipped,
        both, both, both, flipped,
        P(NODES, None), P(NODES), P(NODES, None), P(NODES, None), P(NODES),
    )
    return jax.shard_map(
        local, mesh=fine, in_specs=in_specs, out_specs=(both, both), check_vma=False
    )
```

profile of v0, /device:TPU:128, one launch (start us, length us, event | category | flops | bytes accessed | tf_op | source)
XLA Modules:
  0.0 321.0 jit_solution(8601101025057184230)
XLA Ops:
  7.2 1.8 shard_map.213
  9.0 47.1 %all_to_all.40.src = bf16[16,20,8,128]{3,2,1,0:T(8,128)(2,1)S(1)} all-to-all(bf16[16,20,8,128]{3,2,1,0:T(8,128)(2,1)} %shard_map.213), channel_id=1, replica_groups=mesh['zh'=4,'y'=4,'x'=4,'core'=2,'heads'=4] {'zh','heads'}, dimensions={0} | all-to-all | bytes 1310720 | tf_op jit(solution)/shard_map/all_to_all | solution.py:398
  56.1 1.2 shard_map.214
  57.4 36.9 %all_to_all.41.mine = bf16[16,4,8,1536]{3,2,1,0:T(8,128)(2,1)S(1)} all-to-all(bf16[16,4,8,1536]{3,2,1,0:T(8,128)(2,1)S(1)} %get-tuple-element.14), channel_id=1, replica_groups=mesh['zh'=4,'y'=4,'x'=4,'core'=2,'heads'=4] {'y','x'}, dimensions={0} | all-to-all | bytes 3145728 | tf_op jit(solution)/shard_map/all_to_all | solution.py:357
  94.2 1.9 collective-permute-start.3
  96.2 1.1 dynamic-slice_bitcast_fusion
  97.3 0.7 pad_maximum_fusion
  97.9 3.9 %collective-permute-start = (bf16[320,256]{1,0:T(8,128)(2,1)}, bf16[320,256]{1,0:T(8,128)(2,1)S(1)}, u32[]{:S(2)}, u32[]{:S(2)}) collective-permute-start(bf16[320,256]{1,0:T(8,128)(2,1)} %pad_maximum_fusion), channel_id=1, source_target_pairs={{0,1},{1,0},{2,3},{3,2},{4,5},{5,4},{6,7},{7,6},{8,9},{9,8},{10,11... | collective-permute-start | bytes 491528 | tf_op jit(solution)/shard_map/ppermute | solution.py:345
  101.8 0.7 pad_maximum_fusion.1
  102.5 1.9 collective-permute-start.1
  104.4 0.7 pad_maximum_fusion.2
  105.1 4.3 %collective-permute-start.2 = (bf16[320,256]{1,0:T(8,128)(2,1)}, bf16[320,256]{1,0:T(8,128)(2,1)}, u32[]{:S(2)}, u32[]{:S(2)}) collective-permute-start(bf16[320,256]{1,0:T(8,128)(2,1)} %pad_maximum_fusion.2), channel_id=1, source_target_pairs={{0,3},{1,2},{2,1},{3,0},{4,7},{5,6},{6,5},{7,4},{8,11},{9,10},{10,... | collective-permute-start | bytes 491528 | tf_op jit(solution)/shard_map/ppermute | solution.py:345
  109.5 1.0 copy-done.3
  110.5 0.9 copy-done.5
  112.0 6.6 %collective-permute-done.1.x2 = bf16[320,256]{1,0:T(8,128)(2,1)S(1)} collective-permute-done((bf16[320,256]{1,0:T(8,128)(2,1)}, bf16[320,256]{1,0:T(8,128)(2,1)S(1)}, u32[]{:S(2)}, u32[]{:S(2)}) %collective-permute-start.1) | collective-permute-done | bytes 163872 | tf_op jit(solution)/shard_map/ppermute | solution.py:345
  118.6 1.2 copy-done.1
  119.8 1.5 copy-done.2
  121.3 3.3 %shard_map.215 = (bf16[4,288,256]{2,1,0:T(8,128)(2,1)S(1)}, bf16[4,256,256]{2,1,0:T(8,128)(2,1)S(1)}, bf16[4,64,256]{2,1,0:T(8,128)(2,1)S(1)}) custom-call(s32[5]{0:T(128)S(1)} %stack.19.pos, bf16[320,256]{1,0:T(8,128)(2,1)S(1)} %shard_map.212.x0, bf16[320,256]{1,0:T(8,128)(2,1)S(1)} %collective-permute-done.x1, ...), custom_call_target="tpu_custom_call" | custom-call | flops 268435456 | bytes 1048576 | tf_op jit(solution)/shard_map/pallas_call | solution.py:423
  124.5 21.3 %all_to_all.42.own = bf16[4,288,256]{2,1,0:T(8,128)(2,1)S(1)} all-to-all(bf16[4,288,256]{2,1,0:T(8,128)(2,1)S(1)} %get-tuple-element.19), channel_id=1, replica_groups=mesh['zh'=4,'y'=4,'x'=4,'core'=2,'heads'=4] {'heads'}, dimensions={0} | all-to-all | bytes 1179648 | tf_op jit(solution)/shard_map/all_to_all | solution.py:320
  145.9 4.8 %collective-permute-start.5 = (bf16[2,256,256]{2,1,0:T(8,128)(2,1)S(1)}, bf16[2,256,256]{2,1,0:T(8,128)(2,1)S(1)}, u32[]{:S(2)}, u32[]{:S(2)}) collective-permute-start(bf16[2,256,256]{2,1,0:T(8,128)(2,1)S(1)} %get-tuple-element.26), channel_id=1, source_target_pairs={{4,0},{8,4},{12,8},{16,12},{20,16},{24,20},{28,24},{32,28},{36,32}... | collective-permute-start | bytes 786440 | tf_op jit(solution)/shard_map/ppermute | solution.py:327
  150.7 1.9 collective-permute-start.4
  152.6 10.0 %collective-permute-done.5.after = bf16[2,256,256]{2,1,0:T(8,128)(2,1)S(1)} collective-permute-done((bf16[2,256,256]{2,1,0:T(8,128)(2,1)S(1)}, bf16[2,256,256]{2,1,0:T(8,128)(2,1)S(1)}, u32[]{:S(2)}, u32[]{:S(2)}) %collective-permute-start.5) | collective-permute-done | bytes 262176 | tf_op jit(solution)/shard_map/ppermute | solution.py:327
  162.6 4.2 %collective-permute-done.4.before = bf16[2,256,256]{2,1,0:T(8,128)(2,1)S(1)} collective-permute-done((bf16[2,256,256]{2,1,0:T(8,128)(2,1)S(1)}, bf16[2,256,256]{2,1,0:T(8,128)(2,1)S(1)}, u32[]{:S(2)}, u32[]{:S(2)}) %collective-permute-start.4) | collective-permute-done | bytes 262176 | tf_op jit(solution)/shard_map/ppermute | solution.py:327
  166.8 2.0 shard_map.216
  168.8 1.9 collective-permute-start.6
  170.8 1.7 slice.20
  172.5 2.4 collective-permute-start.7
  174.9 16.7 %all_to_all.43.encoded = bf16[4,64,128]{2,1,0:T(8,128)(2,1)S(1)} all-to-all(bf16[4,64,128]{2,1,0:T(8,128)(2,1)S(1)} %shard_map.216), channel_id=1, replica_groups=mesh['zh'=4,'y'=4,'x'=4,'core'=2,'heads'=4] {'heads'}, dimensions={0} | all-to-all | bytes 131072 | tf_op jit(solution)/shard_map/all_to_all | solution.py:320
  191.6 3.5 %shard_map.218 = (bf16[4,64,384]{2,1,0:T(8,128)(2,1)S(1)}, bf16[64,1024]{1,0:T(8,128)(2,1)S(1)}) custom-call(s32[5]{0:T(128)S(1)} %stack.19.pos, bf16[4,64,128]{2,1,0:T(8,128)(2,1)S(1)} %all_to_all.43.encoded, bf16[4,64,256]{2,1,0:T(8,128)(2,1)S(1)} %get-tuple-element.21.mesh, bf16[16,4,8,8704]{3,2,1,0:T(8,128)(2,1)} %bitcast.33, ...), custom_call_target="tpu_custom_call" | custom-call | flops 268435456 | bytes 1048576 | tf_op jit(solution)/shard_map/pallas_call | solution.py:443
  195.2 15.0 %all_to_all.44.own = bf16[4,64,384]{2,1,0:T(8,128)(2,1)S(1)} all-to-all(bf16[4,64,384]{2,1,0:T(8,128)(2,1)S(1)} %get-tuple-element.22), channel_id=1, replica_groups=mesh['zh'=4,'y'=4,'x'=4,'core'=2,'heads'=4] {'heads'}, dimensions={0} | all-to-all | bytes 393216 | tf_op jit(solution)/shard_map/all_to_all | solution.py:320
  210.1 1.9 collective-permute-start.9
  212.1 2.4 collective-permute-start.8
  214.5 3.8 %collective-permute-done.9.after = bf16[4,64,256]{2,1,0:T(8,128)(2,1)S(1)} collective-permute-done((bf16[4,64,256]{2,1,0:T(8,128)(2,1)S(1)}, bf16[4,64,256]{2,1,0:T(8,128)(2,1)S(1)}, u32[]{:S(2)}, u32[]{:S(2)}) %collective-permute-start.9) | collective-permute-done | bytes 131104 | tf_op jit(solution)/shard_map/ppermute | solution.py:327
  218.3 8.3 %collective-permute-done.8.before = bf16[4,64,256]{2,1,0:T(8,128)(2,1)S(1)} collective-permute-done((bf16[4,64,256]{2,1,0:T(8,128)(2,1)S(1)}, bf16[4,64,256]{2,1,0:T(8,128)(2,1)S(1)}, u32[]{:S(2)}, u32[]{:S(2)}) %collective-permute-start.8) | collective-permute-done | bytes 131104 | tf_op jit(solution)/shard_map/ppermute | solution.py:327
  226.6 1.6 shard_map.219
  228.2 12.2 %all_to_all.45.windowed = bf16[4,64,128]{2,1,0:T(8,128)(2,1)S(1)} all-to-all(bf16[4,64,128]{2,1,0:T(8,128)(2,1)S(1)} %shard_map.219), channel_id=1, replica_groups=mesh['zh'=4,'y'=4,'x'=4,'core'=2,'heads'=4] {'heads'}, dimensions={0} | all-to-all | bytes 131072 | tf_op jit(solution)/shard_map/all_to_all | solution.py:320
  240.4 8.5 %shard_map.220 = (bf16[4,64,256]{2,1,0:T(8,128)(2,1)}, bf16[64,1024]{1,0:T(8,128)(2,1)S(1)}) custom-call(s32[5]{0:T(128)S(1)} %stack.19.pos, bf16[4,64,128]{2,1,0:T(8,128)(2,1)S(1)} %all_to_all.45.windowed, bf16[64,1024]{1,0:T(8,128)(2,1)S(1)} %get-tuple-element.23.kept, bf16[16,4,8,8704]{3,2,1,0:T(8,128)(2,1)} %bitcast.34, ...), custom_call_target="tpu_custom_call" | custom-call | flops 268435456 | bytes 1048576 | tf_op jit(solution)/shard_map/pallas_call | solution.py:460
  249.0 3.3 %all-to-all-start.7 = ((bf16[4,64,256]{2,1,0:T(8,128)(2,1)}), bf16[4,64,256]{2,1,0:T(8,128)(2,1)S(1)}, u32[]{:S(2)}, u32[]{:S(2)}) async-start(bf16[4,64,256]{2,1,0:T(8,128)(2,1)} %get-tuple-element.25), calls=%async_computation.7 | async-start | bytes 262144 | tf_op jit(solution)/shard_map/all_to_all | solution.py:320
  252.3 15.3 %all-gather.1 = bf16[256,1024]{1,0:T(8,128)(2,1)S(1)} all-gather(bf16[64,1024]{1,0:T(8,128)(2,1)S(1)} %get-tuple-element.24), channel_id=3, replica_groups=mesh['zh'=4,'y'=4,'x'=4,'core'=2,'heads'=4] {'heads'}, dimensions={0}, use_global_device_ids=true | all-gather | bytes 655360 | tf_op jit(solution)/shard_map/all_gather | solution.py:467
  267.6 1.9 collective-permute-start.11
  269.5 2.6 collective-permute-start.10
  272.2 2.4 shard_map.217.queries
  274.7 7.0 %collective-permute-done.11.after = bf16[128,1024]{1,0:T(8,128)(2,1)S(1)} collective-permute-done((bf16[128,1024]{1,0:T(8,128)(2,1)S(1)}, bf16[128,1024]{1,0:T(8,128)(2,1)S(1)}, u32[]{:S(2)}, u32[]{:S(2)}) %collective-permute-start.11) | collective-permute-done | bytes 262176 | tf_op jit(solution)/shard_map/ppermute | solution.py:327
  281.7 6.1 %collective-permute-done.10.before = bf16[128,1024]{1,0:T(8,128)(2,1)S(1)} collective-permute-done((bf16[128,1024]{1,0:T(8,128)(2,1)S(1)}, bf16[128,1024]{1,0:T(8,128)(2,1)S(1)}, u32[]{:S(2)}, u32[]{:S(2)}) %collective-permute-start.10) | collective-permute-done | bytes 262176 | tf_op jit(solution)/shard_map/ppermute | solution.py:327
  287.7 6.2 %shard_map.221 = bf16[4,256,256]{2,1,0:T(8,128)(2,1)} custom-call(s32[5]{0:T(128)S(1)} %stack.19.pos, s32[8,3]{1,0:T(8,128)S(1)} %copy.24.blocks, s32[8]{0:T(128)S(1)} %copy-done.8, bf16[4,256,256]{2,1,0:T(8,128)(2,1)S(1)} %get-tuple-element.17.grid, bf16[256,512]{1,0:T(8,128)(2,1)S(1)} %shard_map.217.queries, bf16[4,64,1024]{2,1,0:T(8,128)(2,1)S(1)} %bitcast.26, ...), custom_call_target="tpu_custom_call" | custom-call | flops 268435456 | bytes 1048576 | tf_op jit(solution)/shard_map/pallas_call | solution.py:478
  294.0 8.5 %all-to-all-start.6 = ((bf16[4,256,256]{2,1,0:T(8,128)(2,1)}), bf16[4,256,256]{2,1,0:T(8,128)(2,1)S(1)}, u32[]{:S(2)}, u32[]{:S(2)}) async-start(bf16[4,256,256]{2,1,0:T(8,128)(2,1)} %shard_map.221), calls=%async_computation.6 | async-start | bytes 1048576 | tf_op jit(solution)/shard_map/all_to_all | solution.py:320
  302.4 10.3 %all-to-all-done.6 = bf16[4,256,256]{2,1,0:T(8,128)(2,1)S(1)} async-done(((bf16[4,256,256]{2,1,0:T(8,128)(2,1)}), bf16[4,256,256]{2,1,0:T(8,128)(2,1)S(1)}, u32[]{:S(2)}, u32[]{:S(2)}) %all-to-all-start.6) | async-done | bytes 524320 | tf_op jit(solution)/shard_map/all_to_all | solution.py:320
  312.7 0.8 copy.27
  (35 shorter events, 1.6 us)
Async XLA Ops:
  7.2 161.7 %all-gather.4.cloned.1.call-start = ((), (), s32[]{:S(2)}) async-start(), calls=%async_computation.8 | async-start | bytes 9469952 | tf_op jit(solution)/shard_map/all_gather | solution.py:404
  57.3 38.8 %copy-start.4 = (bf16[256,256]{1,0:T(8,128)(2,1)S(1)}, bf16[256,256]{1,0:T(8,128)(2,1)}, u32[]{:S(2)}) copy-start(bf16[256,256]{1,0:T(8,128)(2,1)} %param.22) | copy-start | bytes 393220
  94.2 24.4 %collective-permute-start.3 = (bf16[16,4,8,1536]{3,2,1,0:T(8,128)(2,1)S(1)}, bf16[16,4,8,1536]{3,2,1,0:T(8,128)(2,1)S(1)}, u32[]{:S(2)}, u32[]{:S(2)}) collective-permute-start(bf16[16,4,8,1536]{3,2,1,0:T(8,128)(2,1)S(1)} %all_to_all.41.mine), channel_id=1, source_target_pairs={{0,4},{4,0},{1,5},{5,1},{2,6},{6,2},{3,7},{7,3},{8,12},{12,8},{9,1... | collective-permute-start | bytes 4718600 | tf_op jit(solution)/shard_map/ppermute | solution.py:339
  97.9 14.1 %collective-permute-start = (bf16[320,256]{1,0:T(8,128)(2,1)}, bf16[320,256]{1,0:T(8,128)(2,1)S(1)}, u32[]{:S(2)}, u32[]{:S(2)}) collective-permute-start(bf16[320,256]{1,0:T(8,128)(2,1)} %pad_maximum_fusion), channel_id=1, source_target_pairs={{0,1},{1,0},{2,3},{3,2},{4,5},{5,4},{6,7},{7,6},{8,9},{9,8},{10,11... | collective-permute-start | bytes 491528 | tf_op jit(solution)/shard_map/ppermute | solution.py:345
  102.5 16.1 %collective-permute-start.1 = (bf16[320,256]{1,0:T(8,128)(2,1)}, bf16[320,256]{1,0:T(8,128)(2,1)S(1)}, u32[]{:S(2)}, u32[]{:S(2)}) collective-permute-start(bf16[320,256]{1,0:T(8,128)(2,1)} %pad_maximum_fusion.1), channel_id=1, source_target_pairs={{0,2},{1,3},{2,0},{3,1},{4,6},{5,7},{6,4},{7,5},{8,10},{9,11},{10,... | collective-permute-start | bytes 491528 | tf_op jit(solution)/shard_map/ppermute | solution.py:345
  105.1 13.5 %collective-permute-start.2 = (bf16[320,256]{1,0:T(8,128)(2,1)}, bf16[320,256]{1,0:T(8,128)(2,1)}, u32[]{:S(2)}, u32[]{:S(2)}) collective-permute-start(bf16[320,256]{1,0:T(8,128)(2,1)} %pad_maximum_fusion.2), channel_id=1, source_target_pairs={{0,3},{1,2},{2,1},{3,0},{4,7},{5,6},{6,5},{7,4},{8,11},{9,10},{10,... | collective-permute-start | bytes 491528 | tf_op jit(solution)/shard_map/ppermute | solution.py:345
  109.5 1.0 copy-start.3
  110.5 0.9 copy-start.5
  111.4 55.3 %copy-start.6 = (s32[2,8]{1,0:T(2,128)S(1)}, s32[2,8]{1,0:T(2,128)}, u32[]{:S(2)}) copy-start(s32[2,8]{1,0:T(2,128)} %blocks.2) | copy-start | bytes 196
  111.4 55.3 %copy-start.7 = (s32[2]{0:T(128)S(1)}, s32[2]{0:T(128)}, u32[]{:S(2)}) copy-start(s32[2]{0:T(128)} %count.2) | copy-start | bytes 28
  118.6 1.2 copy-start.1
  119.8 1.5 copy-start.2
  145.9 16.7 %collective-permute-start.5 = (bf16[2,256,256]{2,1,0:T(8,128)(2,1)S(1)}, bf16[2,256,256]{2,1,0:T(8,128)(2,1)S(1)}, u32[]{:S(2)}, u32[]{:S(2)}) collective-permute-start(bf16[2,256,256]{2,1,0:T(8,128)(2,1)S(1)} %get-tuple-element.26), channel_id=1, source_target_pairs={{4,0},{8,4},{12,8},{16,12},{20,16},{24,20},{28,24},{32,28},{36,32}... | collective-permute-start | bytes 786440 | tf_op jit(solution)/shard_map/ppermute | solution.py:327
  150.7 16.1 %collective-permute-start.4 = (bf16[2,256,256]{2,1,0:T(8,128)(2,1)S(1)}, bf16[2,256,256]{2,1,0:T(8,128)(2,1)S(1)}, u32[]{:S(2)}, u32[]{:S(2)}) collective-permute-start(bf16[2,256,256]{2,1,0:T(8,128)(2,1)S(1)} %get-tuple-element.27), channel_id=1, source_target_pairs={{0,4},{4,8},{8,12},{12,16},{16,20},{20,24},{24,28},{28,32},{32,36}... | collective-permute-start | bytes 786440 | tf_op jit(solution)/shard_map/ppermute | solution.py:327
  168.8 71.6 %collective-permute-start.6 = (bf16[16,4,8,8704]{3,2,1,0:T(8,128)(2,1)}, bf16[16,4,8,8704]{3,2,1,0:T(8,128)(2,1)S(1)}, u32[]{:S(2)}, u32[]{:S(2)}) collective-permute-start(bf16[16,4,8,8704]{3,2,1,0:T(8,128)(2,1)} %bitcast.31), channel_id=1, source_target_pairs={{0,4},{4,0},{1,5},{5,1},{2,6},{6,2},{3,7},{7,3},{8,12},{12,8},{9,1... | collective-permute-start | bytes 26738696 | tf_op jit(solution)/shard_map/ppermute | solution.py:339
  172.5 19.2 %collective-permute-start.7 = (bf16[16,4,8,2048]{3,2,1,0:T(8,128)(2,1)S(1)}, bf16[16,4,8,2048]{3,2,1,0:T(8,128)(2,1)S(1)}, u32[]{:S(2)}, u32[]{:S(2)}) collective-permute-start(bf16[16,4,8,2048]{3,2,1,0:T(8,128)(2,1)S(1)} %slice.20), channel_id=1, source_target_pairs={{0,4},{4,0},{1,5},{5,1},{2,6},{6,2},{3,7},{7,3},{8,12},{12,8},{9,1... | collective-permute-start | bytes 6291464 | tf_op jit(solution)/shard_map/ppermute | solution.py:339
  191.6 34.9 %copy-start.9 = (s32[2,4]{1,0:T(2,128)S(1)}, s32[2,4]{1,0:T(2,128)}, u32[]{:S(2)}) copy-start(s32[2,4]{1,0:T(2,128)} %offsets.1) | copy-start | bytes 100
  210.1 8.2 %collective-permute-start.9 = (bf16[4,64,256]{2,1,0:T(8,128)(2,1)S(1)}, bf16[4,64,256]{2,1,0:T(8,128)(2,1)S(1)}, u32[]{:S(2)}, u32[]{:S(2)}) collective-permute-start(bf16[4,64,256]{2,1,0:T(8,128)(2,1)S(1)} %slice.28), channel_id=1, source_target_pairs={{4,0},{8,4},{12,8},{16,12},{20,16},{24,20},{28,24},{32,28},{36,32}... | collective-permute-start | bytes 393224 | tf_op jit(solution)/shard_map/ppermute | solution.py:327
  212.1 14.5 %collective-permute-start.8 = (bf16[4,64,256]{2,1,0:T(8,128)(2,1)S(1)}, bf16[4,64,256]{2,1,0:T(8,128)(2,1)S(1)}, u32[]{:S(2)}, u32[]{:S(2)}) collective-permute-start(bf16[4,64,256]{2,1,0:T(8,128)(2,1)S(1)} %slice.28), channel_id=1, source_target_pairs={{0,4},{4,8},{8,12},{12,16},{16,20},{20,24},{24,28},{28,32},{32,36}... | collective-permute-start | bytes 393224 | tf_op jit(solution)/shard_map/ppermute | solution.py:327
  240.4 8.6 %copy-start = (bf16[16,4,8,8704]{3,2,1,0:T(8,128)(2,1)}, bf16[16,4,8,8704]{3,2,1,0:T(8,128)(2,1)S(1)}, u32[]{:S(2)}) copy-start(bf16[16,4,8,8704]{3,2,1,0:T(8,128)(2,1)S(1)} %collective-permute-done.6.theirs) | copy-start | bytes 26738692
  240.4 31.7 %copy-start.10 = (s32[8,3]{0,1:T(4,128)S(1)}, s32[8,3]{0,1:T(4,128)}, u32[]{:S(2)}) copy-start(s32[8,3]{0,1:T(4,128)} %param.40) | copy-start | bytes 292
  249.0 45.0 %all-to-all-start.7 = ((bf16[4,64,256]{2,1,0:T(8,128)(2,1)}), bf16[4,64,256]{2,1,0:T(8,128)(2,1)S(1)}, u32[]{:S(2)}, u32[]{:S(2)}) async-start(bf16[4,64,256]{2,1,0:T(8,128)(2,1)} %get-tuple-element.25), calls=%async_computation.7 | async-start | bytes 262144 | tf_op jit(solution)/shard_map/all_to_all | solution.py:320
  267.6 14.0 %collective-permute-start.11 = (bf16[128,1024]{1,0:T(8,128)(2,1)S(1)}, bf16[128,1024]{1,0:T(8,128)(2,1)S(1)}, u32[]{:S(2)}, u32[]{:S(2)}) collective-permute-start(bf16[128,1024]{1,0:T(8,128)(2,1)S(1)} %get-tuple-element.28), channel_id=1, source_target_pairs={{4,0},{8,4},{12,8},{16,12},{20,16},{24,20},{28,24},{32,28},{36,32}... | collective-permute-start | bytes 786440 | tf_op jit(solution)/shard_map/ppermute | solution.py:327
  269.5 18.2 %collective-permute-start.10 = (bf16[128,1024]{1,0:T(8,128)(2,1)S(1)}, bf16[128,1024]{1,0:T(8,128)(2,1)S(1)}, u32[]{:S(2)}, u32[]{:S(2)}) collective-permute-start(bf16[128,1024]{1,0:T(8,128)(2,1)S(1)} %get-tuple-element.29), channel_id=1, source_target_pairs={{0,4},{4,8},{8,12},{12,16},{16,20},{20,24},{24,28},{28,32},{32,36}... | collective-permute-start | bytes 786440 | tf_op jit(solution)/shard_map/ppermute | solution.py:327
  272.2 15.5 %copy-start.8 = (s32[8]{0:T(128)S(1)}, s32[8]{0:T(128)}, u32[]{:S(2)}) copy-start(s32[8]{0:T(128)} %count.3) | copy-start | bytes 100
  294.0 18.8 %all-to-all-start.6 = ((bf16[4,256,256]{2,1,0:T(8,128)(2,1)}), bf16[4,256,256]{2,1,0:T(8,128)(2,1)S(1)}, u32[]{:S(2)}, u32[]{:S(2)}) async-start(bf16[4,256,256]{2,1,0:T(8,128)(2,1)} %shard_map.221), calls=%async_computation.6 | async-start | bytes 1048576 | tf_op jit(solution)/shard_map/all_to_all | solution.py:320
Sparse Core Ops, SparseCore 0:
  57.5 88.1 all-gather.3
where the time goes:
time: 322 us; the launch traced here: 321 us
  blocking collectives  164 us (51%)
  waiting for transfers between devices  56.2 us (17%)
  starting transfers between devices  43.7 us (14%)
  Pallas kernels  31.1 us (10%)
  between operations  14.3 us (4%)
  local copies, waits for them, and re-layouts  9.11 us (3%)
    all_to_all x4, blocking collectives, exchange(): return lax.all_to_all(x, 'heads', 0, 0, tiled=True)  65.2 us
    all_to_all x1, blocking collectives, local(): tiles = lax.all_to_all(tiles, ('zh', 'heads'), 0, 0, tiled=True)  47.1 us
    ppermute x6, waiting for transfers between devices, halo(): return (lax.ppermute(last, NODES, up), lax.ppermute(first, NODES, down))  39.3 us
    all_to_all x1, blocking collectives, over_plane(): return lax.all_to_all(x, ('y', 'x'), 0, 0, tiled=True)  36.9 us
    ppermute x6, starting transfers between devices, halo(): return (lax.ppermute(last, NODES, up), lax.ppermute(first, NODES, down))  15.6 us
    all_gather x1, blocking collectives, local(): own = lax.all_gather(spread, 'heads')  15.3 us
    all_to_all x2, starting transfers between devices, exchange(): return lax.all_to_all(x, 'heads', 0, 0, tiled=True)  11.8 us
    all_to_all x2, waiting for transfers between devices, exchange(): return lax.all_to_all(x, 'heads', 0, 0, tiled=True)  10.3 us
  transfers between devices with their start and end apart: 15, of which 8 were waited for; matrix products, arithmetic and copies ran while one was open for 2% of the time, Pallas kernels for 6%

commit v1 on v0

--- a/solution.py
+++ b/solution.py
@@ -278,14 +278,15 @@
     out[...] = (mm(normalize(wide(grid)), weights.get(0)) * SCALE).astype(BF16)
 
 
-def decode_kernel(pos, blocks, count, grid, queries, own, before, after, mine, theirs, out, wo,
-                  tiles, picked, sems):
+def decode_kernel(pos, blocks, count, grid, queries, own, r0, r1, r2, r3, mine, theirs, out, wo,
+                  tiles, sides, picked, sems):
     weights = Weights(CHUNK_B, (10,), pos, mine, theirs, (wo,), sems)
-    tiles[0] = before[...]
+    for k, part in enumerate((r0, r1, r2, r3)):
+        sides[pos[2] ^ k] = part[...]
     for j in range(4):
         half = slice((j % 2) * 64, (j % 2) * 64 + 64)
         tiles[1 + j // 2, half] = own[j]
-    tiles[3] = after[...]
+        tiles[0 if j >= 2 else 3, half] = sides[j]
     start = pos[0] * 2 - 1
     slots = blocks.shape[1]
     column = lax.broadcasted_iota(jnp.int32, (2 * TILE, slots * TILE), 1)
@@ -329,6 +330,13 @@
 
 def after_it(x, other):
     return lax.optimization_barrier((x, other))[0]
+
+
+def beside(rows):
+    size = lax.axis_size(NODES)
+    up = [(n * 4 + j, (n + 1) * 4 + j) for n in range(size - 1) for j in (2, 3)]
+    down = [((n + 1) * 4 + j, n * 4 + j) for n in range(size - 1) for j in (0, 1)]
+    return lax.ppermute(rows, (*NODES, "heads"), up + down)
 
 
 def in_hbm(x):
@@ -450,6 +458,13 @@
     own = exchange(sent)
     side = own[:, :, PAIR:]
     before, after = halo(side, side)
+    (queries,) = call(
+        queries_kernel,
+        [(256, 512)],
+        [in_smem(), in_vmem()] + [in_any()] * 2,
+        weight_scratch(CHUNK_B, (9,)),
+        room=12,
+    )(pos, grid, mine, late)
     (sent,) = call(
         window_kernel,
         [(4, 64, 128)],
@@ -463,26 +478,25 @@
         [in_smem(), in_vmem(), in_vmem()] + [in_any()] * 2,
         weight_scratch(CHUNK_B, (4, 5, 6, 7, 8)),
         room=24,
-    )(pos, windowed, kept, mine, theirs)
+    )(pos, windowed, kept, mine, late)
+    arrived = beside(spread)
     own = lax.all_gather(spread, "heads")
-    before, after = halo(own[2:].reshape(TILE, D), own[:2].reshape(TILE, D))
+    sides = trade([after_it(arrived, own)] * 4)
     mesh_out = exchange(sent).reshape(256, 256)
-    (queries,) = call(
-        queries_kernel,
-        [(256, 512)],
-        [in_smem(), in_vmem()] + [in_any()] * 2,
-        weight_scratch(CHUNK_B, (9,)),
-        room=12,
-    )(pos, grid, mine, late)
     last = weight_scratch(CHUNK_B, (10,))
     (sent,) = call(
         decode_kernel,
         [(4, 256, 256)],
-        [in_smem()] * 3 + [in_vmem()] * 5 + [in_any()] * 2,
+        [in_smem()] * 3 + [in_vmem()] * 7 + [in_any()] * 2,
         last[:-1]
-        + [pltpu.VMEM((4, TILE, D), BF16), pltpu.VMEM((3 * TILE, D), BF16), last[-1]],
+        + [
+            pltpu.VMEM((4, TILE, D), BF16),
+            pltpu.VMEM((4, 64, D), BF16),
+            pltpu.VMEM((3 * TILE, D), BF16),
+            last[-1],
+        ],
         room=16,
-    )(pos, decoder_blocks, decoder_count, grid, queries, own, before, after, mine, late)
+    )(pos, decoder_blocks, decoder_count, grid, queries, own, *sides, mine, late)
     grid_out = exchange(sent).reshape(1024, 256)
     return grid_out, mesh_out
 

time: 322 us -> 320 us (level)
  waiting for transfers between devices: 56.2 us -> 47.2 us
  local copies, waits for them, and re-layouts: 9.11 us -> 12.6 us
    ppermute x6 -> x4, waiting for transfers between devices: 39.3 us -> 26.2 us  [halo(): return (lax.ppermute(last, NODES, up), lax.ppermute(first, NODES, down))]
    ppermute x3 -> x6, starting transfers between devices: 10.1 us -> 20.4 us  [trade(): out.append(lax.ppermute(parts[k], 'heads', [(i, i ^ k) for i in range(4)]))]
    all_to_all x2, starting transfers between devices: 11.8 us -> 6.82 us  [exchange(): return lax.all_to_all(x, 'heads', 0, 0, tiled=True)]
    ppermute x6 -> x4, starting transfers between devices: 15.6 us -> 11.1 us  [halo(): return (lax.ppermute(last, NODES, up), lax.ppermute(first, NODES, down))]
    unnamed x25, local copies, waits for them, and re-layouts: 6.14 us -> 9.62 us
    ppermute x3 -> x6, waiting for transfers between devices: 6.59 us -> 8.45 us  [trade(): out.append(lax.ppermute(parts[k], 'heads', [(i, i ^ k) for i in range(4)]))]
  transfers between devices with their start and end apart: 15 -> 17, of which waited for: 8 -> 8; matrix products, arithmetic and copies ran while one was open for 2% -> 2% of each run, Pallas kernels for 6% -> 6%
where the time goes in v1:
time: 320 us; the launch traced here: 319 us
  blocking collectives  167 us (52%)
  waiting for transfers between devices  47.2 us (15%)
  starting transfers between devices  46.4 us (14%)
  Pallas kernels  29.9 us (9%)
  between operations  14.3 us (4%)
  local copies, waits for them, and re-layouts  12.6 us (4%)
    all_to_all x4, blocking collectives, exchange(): return lax.all_to_all(x, 'heads', 0, 0, tiled=True)  65.2 us
    all_to_all x1, blocking collectives, local(): tiles = lax.all_to_all(tiles, ('zh', 'heads'), 0, 0, tiled=True)  47.1 us
    all_to_all x1, blocking collectives, over_plane(): return lax.all_to_all(x, ('y', 'x'), 0, 0, tiled=True)  36.9 us
    ppermute x4, waiting for transfers between devices, halo(): return (lax.ppermute(last, NODES, up), lax.ppermute(first, NODES, down))  26.2 us
    ppermute x6, starting transfers between devices, trade(): out.append(lax.ppermute(parts[k], 'heads', [(i, i ^ k) for i in range(4)]))  20.4 us
    all_gather x1, blocking collectives, local(): own = lax.all_gather(spread, 'heads')  17.4 us
    all_to_all x2, waiting for transfers between devices, exchange(): return lax.all_to_all(x, 'heads', 0, 0, tiled=True)  12.5 us
    ppermute x4, starting transfers between devices, halo(): return (lax.ppermute(last, NODES, up), lax.ppermute(first, NODES, down))  11.1 us
  transfers between devices with their start and end apart: 17, of which 8 were waited for; matrix products, arithmetic and copies ran while one was open for 2% of the time, Pallas kernels for 6%

profile of v1, /device:TPU:128, one launch (start us, length us, event | category | flops | bytes accessed | tf_op | source)
XLA Modules:
  0.0 319.0 jit_solution(16808947609363405803)
XLA Ops:
  7.2 1.8 shard_map.213
  9.0 47.1 %all_to_all.40.src = bf16[16,20,8,128]{3,2,1,0:T(8,128)(2,1)S(1)} all-to-all(bf16[16,20,8,128]{3,2,1,0:T(8,128)(2,1)} %shard_map.213), channel_id=1, replica_groups=mesh['zh'=4,'y'=4,'x'=4,'core'=2,'heads'=4] {'zh','heads'}, dimensions={0} | all-to-all | bytes 1310720 | tf_op jit(solution)/shard_map/all_to_all | solution.py:406
  56.1 1.2 shard_map.214
  57.4 36.9 %all_to_all.41.mine = bf16[16,4,8,1536]{3,2,1,0:T(8,128)(2,1)S(1)} all-to-all(bf16[16,4,8,1536]{3,2,1,0:T(8,128)(2,1)S(1)} %get-tuple-element.15), channel_id=1, replica_groups=mesh['zh'=4,'y'=4,'x'=4,'core'=2,'heads'=4] {'y','x'}, dimensions={0} | all-to-all | bytes 3145728 | tf_op jit(solution)/shard_map/all_to_all | solution.py:365
  94.2 1.9 collective-permute-start.3
  96.2 1.1 dynamic-slice_bitcast_fusion
  97.9 3.9 %collective-permute-start = (bf16[320,256]{1,0:T(8,128)(2,1)}, bf16[320,256]{1,0:T(8,128)(2,1)S(1)}, u32[]{:S(2)}, u32[]{:S(2)}) collective-permute-start(bf16[320,256]{1,0:T(8,128)(2,1)} %pad_maximum_fusion), channel_id=1, source_target_pairs={{0,1},{1,0},{2,3},{3,2},{4,5},{5,4},{6,7},{7,6},{8,9},{9,8},{10,11... | collective-permute-start | bytes 491528 | tf_op jit(solution)/shard_map/ppermute | solution.py:353
  102.5 1.9 collective-permute-start.1
  104.4 0.7 pad_maximum_fusion.2
  105.1 4.3 %collective-permute-start.2 = (bf16[320,256]{1,0:T(8,128)(2,1)}, bf16[320,256]{1,0:T(8,128)(2,1)}, u32[]{:S(2)}, u32[]{:S(2)}) collective-permute-start(bf16[320,256]{1,0:T(8,128)(2,1)} %pad_maximum_fusion.2), channel_id=1, source_target_pairs={{0,3},{1,2},{2,1},{3,0},{4,7},{5,6},{6,5},{7,4},{8,11},{9,10},{10,... | collective-permute-start | bytes 491528 | tf_op jit(solution)/shard_map/ppermute | solution.py:353
  109.5 1.0 copy-done.2
  110.5 0.9 copy-done.4
  112.0 6.6 %collective-permute-done.1.x2 = bf16[320,256]{1,0:T(8,128)(2,1)S(1)} collective-permute-done((bf16[320,256]{1,0:T(8,128)(2,1)}, bf16[320,256]{1,0:T(8,128)(2,1)S(1)}, u32[]{:S(2)}, u32[]{:S(2)}) %collective-permute-start.1) | collective-permute-done | bytes 163872 | tf_op jit(solution)/shard_map/ppermute | solution.py:353
  118.6 1.2 copy-done
  119.8 1.5 copy-done.1
  121.3 3.3 %shard_map.215 = (bf16[4,288,256]{2,1,0:T(8,128)(2,1)S(1)}, bf16[4,256,256]{2,1,0:T(8,128)(2,1)S(1)}, bf16[4,64,256]{2,1,0:T(8,128)(2,1)S(1)}) custom-call(s32[5]{0:T(128)S(1)} %stack.19.pos, bf16[320,256]{1,0:T(8,128)(2,1)S(1)} %shard_map.212.x0, bf16[320,256]{1,0:T(8,128)(2,1)S(1)} %collective-permute-done.x1, ...), custom_call_target="tpu_custom_call" | custom-call | flops 268435456 | bytes 1048576 | tf_op jit(solution)/shard_map/pallas_call | solution.py:431
  124.6 21.3 %all_to_all.42.own = bf16[4,288,256]{2,1,0:T(8,128)(2,1)S(1)} all-to-all(bf16[4,288,256]{2,1,0:T(8,128)(2,1)S(1)} %get-tuple-element.20), channel_id=1, replica_groups=mesh['zh'=4,'y'=4,'x'=4,'core'=2,'heads'=4] {'heads'}, dimensions={0} | all-to-all | bytes 1179648 | tf_op jit(solution)/shard_map/all_to_all | solution.py:321
  145.9 4.8 %collective-permute-start.5 = (bf16[2,256,256]{2,1,0:T(8,128)(2,1)S(1)}, bf16[2,256,256]{2,1,0:T(8,128)(2,1)S(1)}, u32[]{:S(2)}, u32[]{:S(2)}) collective-permute-start(bf16[2,256,256]{2,1,0:T(8,128)(2,1)S(1)} %get-tuple-element.28), channel_id=1, source_target_pairs={{4,0},{8,4},{12,8},{16,12},{20,16},{24,20},{28,24},{32,28},{36,32}... | collective-permute-start | bytes 786440 | tf_op jit(solution)/shard_map/ppermute | solution.py:328
  150.7 1.9 collective-permute-start.4
  152.6 9.9 %collective-permute-done.5.after = bf16[2,256,256]{2,1,0:T(8,128)(2,1)S(1)} collective-permute-done((bf16[2,256,256]{2,1,0:T(8,128)(2,1)S(1)}, bf16[2,256,256]{2,1,0:T(8,128)(2,1)S(1)}, u32[]{:S(2)}, u32[]{:S(2)}) %collective-permute-start.5) | collective-permute-done | bytes 262176 | tf_op jit(solution)/shard_map/ppermute | solution.py:328
  162.5 4.3 %collective-permute-done.4.before = bf16[2,256,256]{2,1,0:T(8,128)(2,1)S(1)} collective-permute-done((bf16[2,256,256]{2,1,0:T(8,128)(2,1)S(1)}, bf16[2,256,256]{2,1,0:T(8,128)(2,1)S(1)}, u32[]{:S(2)}, u32[]{:S(2)}) %collective-permute-start.4) | collective-permute-done | bytes 262176 | tf_op jit(solution)/shard_map/ppermute | solution.py:328
  166.8 2.0 shard_map.216
  168.8 1.9 collective-permute-start.6
  170.8 1.7 slice.14
  172.5 2.4 collective-permute-start.7
  174.9 16.7 %all_to_all.43.encoded = bf16[4,64,128]{2,1,0:T(8,128)(2,1)S(1)} all-to-all(bf16[4,64,128]{2,1,0:T(8,128)(2,1)S(1)} %shard_map.216), channel_id=1, replica_groups=mesh['zh'=4,'y'=4,'x'=4,'core'=2,'heads'=4] {'heads'}, dimensions={0} | all-to-all | bytes 131072 | tf_op jit(solution)/shard_map/all_to_all | solution.py:321
  191.7 3.5 %shard_map.218 = (bf16[4,64,384]{2,1,0:T(8,128)(2,1)S(1)}, bf16[64,1024]{1,0:T(8,128)(2,1)S(1)}) custom-call(s32[5]{0:T(128)S(1)} %stack.19.pos, bf16[4,64,128]{2,1,0:T(8,128)(2,1)S(1)} %all_to_all.43.encoded, bf16[4,64,256]{2,1,0:T(8,128)(2,1)S(1)} %get-tuple-element.22.mesh, bf16[16,4,8,8704]{3,2,1,0:T(8,128)(2,1)} %bitcast.33, ...), custom_call_target="tpu_custom_call" | custom-call | flops 268435456 | bytes 1048576 | tf_op jit(solution)/shard_map/pallas_call | solution.py:451
  195.2 15.0 %all_to_all.44.own = bf16[4,64,384]{2,1,0:T(8,128)(2,1)S(1)} all-to-all(bf16[4,64,384]{2,1,0:T(8,128)(2,1)S(1)} %get-tuple-element.23), channel_id=1, replica_groups=mesh['zh'=4,'y'=4,'x'=4,'core'=2,'heads'=4] {'heads'}, dimensions={0} | all-to-all | bytes 393216 | tf_op jit(solution)/shard_map/all_to_all | solution.py:321
  210.1 1.9 collective-permute-start.9
  212.1 2.4 collective-permute-start.8
  214.5 3.8 %collective-permute-done.9.after = bf16[4,64,256]{2,1,0:T(8,128)(2,1)S(1)} collective-permute-done((bf16[4,64,256]{2,1,0:T(8,128)(2,1)S(1)}, bf16[4,64,256]{2,1,0:T(8,128)(2,1)S(1)}, u32[]{:S(2)}, u32[]{:S(2)}) %collective-permute-start.9) | collective-permute-done | bytes 131104 | tf_op jit(solution)/shard_map/ppermute | solution.py:328
  218.3 8.3 %collective-permute-done.8.before = bf16[4,64,256]{2,1,0:T(8,128)(2,1)S(1)} collective-permute-done((bf16[4,64,256]{2,1,0:T(8,128)(2,1)S(1)}, bf16[4,64,256]{2,1,0:T(8,128)(2,1)S(1)}, u32[]{:S(2)}, u32[]{:S(2)}) %collective-permute-start.8) | collective-permute-done | bytes 131104 | tf_op jit(solution)/shard_map/ppermute | solution.py:328
  226.6 1.6 shard_map.219
  228.2 12.2 %all_to_all.45.windowed = bf16[4,64,128]{2,1,0:T(8,128)(2,1)S(1)} all-to-all(bf16[4,64,128]{2,1,0:T(8,128)(2,1)S(1)} %shard_map.219), channel_id=1, replica_groups=mesh['zh'=4,'y'=4,'x'=4,'core'=2,'heads'=4] {'heads'}, dimensions={0} | all-to-all | bytes 131072 | tf_op jit(solution)/shard_map/all_to_all | solution.py:321
  240.4 3.5 %copy-done.9 = bf16[16,4,8,8704]{3,2,1,0:T(8,128)(2,1)} copy-done((bf16[16,4,8,8704]{3,2,1,0:T(8,128)(2,1)}, bf16[16,4,8,8704]{3,2,1,0:T(8,128)(2,1)S(1)}, u32[]{:S(2)}) %copy-start.9) | copy-done | bytes 8912920
  243.9 7.3 %shard_map.220 = (bf16[4,64,256]{2,1,0:T(8,128)(2,1)}, bf16[64,1024]{1,0:T(8,128)(2,1)S(1)}) custom-call(s32[5]{0:T(128)S(1)} %stack.19.pos, bf16[4,64,128]{2,1,0:T(8,128)(2,1)S(1)} %all_to_all.45.windowed, bf16[64,1024]{1,0:T(8,128)(2,1)S(1)} %get-tuple-element.24.kept, bf16[16,4,8,8704]{3,2,1,0:T(8,128)(2,1)} %bitcast.34, bf16[16,4,8,8704]{3,2,1,0:T(8,128)(2,1)} %copy-done.9), custom_call_target="tpu_custom_call" | custom-call | flops 268435456 | bytes 1048576 | tf_op jit(solution)/shard_map/pallas_call | solution.py:475
  251.2 3.3 %all-to-all-start.7 = ((bf16[4,64,256]{2,1,0:T(8,128)(2,1)}), bf16[4,64,256]{2,1,0:T(8,128)(2,1)S(1)}, u32[]{:S(2)}, u32[]{:S(2)}) async-start(bf16[4,64,256]{2,1,0:T(8,128)(2,1)} %get-tuple-element.27), calls=%async_computation.7 | async-start | bytes 262144 | tf_op jit(solution)/shard_map/all_to_all | solution.py:321
  254.5 1.9 collective-permute-start.10
  256.4 17.4 %all-gather.1 = bf16[256,1024]{1,0:T(8,128)(2,1)S(1)} all-gather(bf16[64,1024]{1,0:T(8,128)(2,1)S(1)} %get-tuple-element.25), channel_id=3, replica_groups=mesh['zh'=4,'y'=4,'x'=4,'core'=2,'heads'=4] {'heads'}, dimensions={0}, use_global_device_ids=true | all-gather | bytes 655360 | tf_op jit(solution)/shard_map/all_gather | solution.py:483
  273.8 4.1 %collective-permute-start.13 = (bf16[64,1024]{1,0:T(8,128)(2,1)S(1)}, bf16[64,1024]{1,0:T(8,128)(2,1)S(1)}, u32[]{:S(2)}, u32[]{:S(2)}) collective-permute-start(bf16[64,1024]{1,0:T(8,128)(2,1)S(1)} %collective-permute-done.10.r0), channel_id=1, source_target_pairs={{0,3},{1,2},{2,1},{3,0},{4,7},{5,6},{6,5},{7,4},{8,11},{9,10},{10,... | collective-permute-start | bytes 393224 | tf_op jit(solution)/shard_map/ppermute | solution.py:353
  277.9 1.9 collective-permute-start.12
  279.9 4.2 %collective-permute-start.11 = (bf16[64,1024]{1,0:T(8,128)(2,1)S(1)}, bf16[64,1024]{1,0:T(8,128)(2,1)S(1)}, u32[]{:S(2)}, u32[]{:S(2)}) collective-permute-start(bf16[64,1024]{1,0:T(8,128)(2,1)S(1)} %collective-permute-done.10.r0), channel_id=1, source_target_pairs={{0,1},{1,0},{2,3},{3,2},{4,5},{5,4},{6,7},{7,6},{8,9},{9,8},{10,11... | collective-permute-start | bytes 393224 | tf_op jit(solution)/shard_map/ppermute | solution.py:353
  284.2 2.4 shard_map.217.queries
  287.3 1.2 collective-permute-done.11.r1
  288.5 6.3 %shard_map.221 = bf16[4,256,256]{2,1,0:T(8,128)(2,1)} custom-call(s32[5]{0:T(128)S(1)} %stack.19.pos, s32[8,3]{1,0:T(8,128)S(1)} %copy.24.blocks, s32[8]{0:T(128)S(1)} %copy-done.7, bf16[4,256,256]{2,1,0:T(8,128)(2,1)S(1)} %get-tuple-element.18.grid, bf16[256,512]{1,0:T(8,128)(2,1)S(1)} %shard_map.217.queries, bf16[4,64,1024]{2,1,0:T(8,128)(2,1)S(1)} %bitcast.26, ...), custom_call_target="tpu_custom_call" | custom-call | flops 268435456 | bytes 1048576 | tf_op jit(solution)/shard_map/pallas_call | solution.py:487
  294.8 3.5 %all-to-all-start.6 = ((bf16[4,256,256]{2,1,0:T(8,128)(2,1)}), bf16[4,256,256]{2,1,0:T(8,128)(2,1)S(1)}, u32[]{:S(2)}, u32[]{:S(2)}) async-start(bf16[4,256,256]{2,1,0:T(8,128)(2,1)} %shard_map.221), calls=%async_computation.6 | async-start | bytes 1048576 | tf_op jit(solution)/shard_map/all_to_all | solution.py:321
  298.3 12.5 %all-to-all-done.6 = bf16[4,256,256]{2,1,0:T(8,128)(2,1)S(1)} async-done(((bf16[4,256,256]{2,1,0:T(8,128)(2,1)}), bf16[4,256,256]{2,1,0:T(8,128)(2,1)S(1)}, u32[]{:S(2)}, u32[]{:S(2)}) %all-to-all-start.6) | async-done | bytes 524320 | tf_op jit(solution)/shard_map/all_to_all | solution.py:321
  310.7 0.8 copy.27
  (38 shorter events, 3.6 us)
Async XLA Ops:
  7.2 161.7 %all-gather.4.cloned.1.call-start = ((), (), s32[]{:S(2)}) async-start(), calls=%async_computation.8 | async-start | bytes 9469952 | tf_op jit(solution)/shard_map/all_gather | solution.py:412
  57.3 38.8 %copy-start.3 = (bf16[256,256]{1,0:T(8,128)(2,1)S(1)}, bf16[256,256]{1,0:T(8,128)(2,1)}, u32[]{:S(2)}) copy-start(bf16[256,256]{1,0:T(8,128)(2,1)} %param.22) | copy-start | bytes 393220
  94.2 24.4 %collective-permute-start.3 = (bf16[16,4,8,1536]{3,2,1,0:T(8,128)(2,1)S(1)}, bf16[16,4,8,1536]{3,2,1,0:T(8,128)(2,1)S(1)}, u32[]{:S(2)}, u32[]{:S(2)}) collective-permute-start(bf16[16,4,8,1536]{3,2,1,0:T(8,128)(2,1)S(1)} %all_to_all.41.mine), channel_id=1, source_target_pairs={{0,4},{4,0},{1,5},{5,1},{2,6},{6,2},{3,7},{7,3},{8,12},{12,8},{9,1... | collective-permute-start | bytes 4718600 | tf_op jit(solution)/shard_map/ppermute | solution.py:347
  97.9 14.1 %collective-permute-start = (bf16[320,256]{1,0:T(8,128)(2,1)}, bf16[320,256]{1,0:T(8,128)(2,1)S(1)}, u32[]{:S(2)}, u32[]{:S(2)}) collective-permute-start(bf16[320,256]{1,0:T(8,128)(2,1)} %pad_maximum_fusion), channel_id=1, source_target_pairs={{0,1},{1,0},{2,3},{3,2},{4,5},{5,4},{6,7},{7,6},{8,9},{9,8},{10,11... | collective-permute-start | bytes 491528 | tf_op jit(solution)/shard_map/ppermute | solution.py:353
  102.5 16.1 %collective-permute-start.1 = (bf16[320,256]{1,0:T(8,128)(2,1)}, bf16[320,256]{1,0:T(8,128)(2,1)S(1)}, u32[]{:S(2)}, u32[]{:S(2)}) collective-permute-start(bf16[320,256]{1,0:T(8,128)(2,1)} %pad_maximum_fusion.1), channel_id=1, source_target_pairs={{0,2},{1,3},{2,0},{3,1},{4,6},{5,7},{6,4},{7,5},{8,10},{9,11},{10,... | collective-permute-start | bytes 491528 | tf_op jit(solution)/shard_map/ppermute | solution.py:353
  105.1 13.5 %collective-permute-start.2 = (bf16[320,256]{1,0:T(8,128)(2,1)}, bf16[320,256]{1,0:T(8,128)(2,1)}, u32[]{:S(2)}, u32[]{:S(2)}) collective-permute-start(bf16[320,256]{1,0:T(8,128)(2,1)} %pad_maximum_fusion.2), channel_id=1, source_target_pairs={{0,3},{1,2},{2,1},{3,0},{4,7},{5,6},{6,5},{7,4},{8,11},{9,10},{10,... | collective-permute-start | bytes 491528 | tf_op jit(solution)/shard_map/ppermute | solution.py:353
  109.5 1.0 copy-start.2
  110.5 0.9 copy-start.4
  111.4 55.3 %copy-start.5 = (s32[2,8]{1,0:T(2,128)S(1)}, s32[2,8]{1,0:T(2,128)}, u32[]{:S(2)}) copy-start(s32[2,8]{1,0:T(2,128)} %blocks.2) | copy-start | bytes 196
  111.4 55.3 %copy-start.6 = (s32[2]{0:T(128)S(1)}, s32[2]{0:T(128)}, u32[]{:S(2)}) copy-start(s32[2]{0:T(128)} %count.2) | copy-start | bytes 28
  118.6 1.2 copy-start
  119.8 1.5 copy-start.1
  145.9 16.6 %collective-permute-start.5 = (bf16[2,256,256]{2,1,0:T(8,128)(2,1)S(1)}, bf16[2,256,256]{2,1,0:T(8,128)(2,1)S(1)}, u32[]{:S(2)}, u32[]{:S(2)}) collective-permute-start(bf16[2,256,256]{2,1,0:T(8,128)(2,1)S(1)} %get-tuple-element.28), channel_id=1, source_target_pairs={{4,0},{8,4},{12,8},{16,12},{20,16},{24,20},{28,24},{32,28},{36,32}... | collective-permute-start | bytes 786440 | tf_op jit(solution)/shard_map/ppermute | solution.py:328
  150.7 16.1 %collective-permute-start.4 = (bf16[2,256,256]{2,1,0:T(8,128)(2,1)S(1)}, bf16[2,256,256]{2,1,0:T(8,128)(2,1)S(1)}, u32[]{:S(2)}, u32[]{:S(2)}) collective-permute-start(bf16[2,256,256]{2,1,0:T(8,128)(2,1)S(1)} %get-tuple-element.29), channel_id=1, source_target_pairs={{0,4},{4,8},{8,12},{12,16},{16,20},{20,24},{24,28},{28,32},{32,36}... | collective-permute-start | bytes 786440 | tf_op jit(solution)/shard_map/ppermute | solution.py:328
  168.8 71.6 %collective-permute-start.6 = (bf16[16,4,8,8704]{3,2,1,0:T(8,128)(2,1)}, bf16[16,4,8,8704]{3,2,1,0:T(8,128)(2,1)S(1)}, u32[]{:S(2)}, u32[]{:S(2)}) collective-permute-start(bf16[16,4,8,8704]{3,2,1,0:T(8,128)(2,1)} %bitcast.31), channel_id=1, source_target_pairs={{0,4},{4,0},{1,5},{5,1},{2,6},{6,2},{3,7},{7,3},{8,12},{12,8},{9,1... | collective-permute-start | bytes 26738696 | tf_op jit(solution)/shard_map/ppermute | solution.py:347
  172.5 19.2 %collective-permute-start.7 = (bf16[16,4,8,2048]{3,2,1,0:T(8,128)(2,1)S(1)}, bf16[16,4,8,2048]{3,2,1,0:T(8,128)(2,1)S(1)}, u32[]{:S(2)}, u32[]{:S(2)}) collective-permute-start(bf16[16,4,8,2048]{3,2,1,0:T(8,128)(2,1)S(1)} %slice.14), channel_id=1, source_target_pairs={{0,4},{4,0},{1,5},{5,1},{2,6},{6,2},{3,7},{7,3},{8,12},{12,8},{9,1... | collective-permute-start | bytes 6291464 | tf_op jit(solution)/shard_map/ppermute | solution.py:347
  191.7 34.9 %copy-start.8 = (s32[2,4]{1,0:T(2,128)S(1)}, s32[2,4]{1,0:T(2,128)}, u32[]{:S(2)}) copy-start(s32[2,4]{1,0:T(2,128)} %offsets.1) | copy-start | bytes 100
  210.1 8.2 %collective-permute-start.9 = (bf16[4,64,256]{2,1,0:T(8,128)(2,1)S(1)}, bf16[4,64,256]{2,1,0:T(8,128)(2,1)S(1)}, u32[]{:S(2)}, u32[]{:S(2)}) collective-permute-start(bf16[4,64,256]{2,1,0:T(8,128)(2,1)S(1)} %slice.18), channel_id=1, source_target_pairs={{4,0},{8,4},{12,8},{16,12},{20,16},{24,20},{28,24},{32,28},{36,32}... | collective-permute-start | bytes 393224 | tf_op jit(solution)/shard_map/ppermute | solution.py:328
  212.1 14.5 %collective-permute-start.8 = (bf16[4,64,256]{2,1,0:T(8,128)(2,1)S(1)}, bf16[4,64,256]{2,1,0:T(8,128)(2,1)S(1)}, u32[]{:S(2)}, u32[]{:S(2)}) collective-permute-start(bf16[4,64,256]{2,1,0:T(8,128)(2,1)S(1)} %slice.18), channel_id=1, source_target_pairs={{0,4},{4,8},{8,12},{12,16},{16,20},{20,24},{24,28},{28,32},{32,36}... | collective-permute-start | bytes 393224 | tf_op jit(solution)/shard_map/ppermute | solution.py:328
  240.4 3.5 %copy-start.9 = (bf16[16,4,8,8704]{3,2,1,0:T(8,128)(2,1)}, bf16[16,4,8,8704]{3,2,1,0:T(8,128)(2,1)S(1)}, u32[]{:S(2)}) copy-start(bf16[16,4,8,8704]{3,2,1,0:T(8,128)(2,1)S(1)} %collective-permute-done.6.theirs) | copy-start | bytes 26738692
  243.9 40.2 %copy-start.10 = (s32[8,3]{0,1:T(4,128)S(1)}, s32[8,3]{0,1:T(4,128)}, u32[]{:S(2)}) copy-start(s32[8,3]{0,1:T(4,128)} %param.40) | copy-start | bytes 292
  251.2 43.6 %all-to-all-start.7 = ((bf16[4,64,256]{2,1,0:T(8,128)(2,1)}), bf16[4,64,256]{2,1,0:T(8,128)(2,1)S(1)}, u32[]{:S(2)}, u32[]{:S(2)}) async-start(bf16[4,64,256]{2,1,0:T(8,128)(2,1)} %get-tuple-element.27), calls=%async_computation.7 | async-start | bytes 262144 | tf_op jit(solution)/shard_map/all_to_all | solution.py:321
  254.5 19.3 %collective-permute-start.10 = (bf16[64,1024]{1,0:T(8,128)(2,1)S(1)}, bf16[64,1024]{1,0:T(8,128)(2,1)S(1)}, u32[]{:S(2)}, u32[]{:S(2)}) collective-permute-start(bf16[64,1024]{1,0:T(8,128)(2,1)S(1)} %get-tuple-element.25), channel_id=1, source_target_pairs={{2,6},{3,7},{6,10},{7,11},{10,14},{11,15},{14,18},{15,19},{18,22},... | collective-permute-start | bytes 393224 | tf_op jit(solution)/shard_map/ppermute | solution.py:339
  273.8 12.8 %collective-permute-start.13 = (bf16[64,1024]{1,0:T(8,128)(2,1)S(1)}, bf16[64,1024]{1,0:T(8,128)(2,1)S(1)}, u32[]{:S(2)}, u32[]{:S(2)}) collective-permute-start(bf16[64,1024]{1,0:T(8,128)(2,1)S(1)} %collective-permute-done.10.r0), channel_id=1, source_target_pairs={{0,3},{1,2},{2,1},{3,0},{4,7},{5,6},{6,5},{7,4},{8,11},{9,10},{10,... | collective-permute-start | bytes 393224 | tf_op jit(solution)/shard_map/ppermute | solution.py:353
  277.9 9.3 %collective-permute-start.12 = (bf16[64,1024]{1,0:T(8,128)(2,1)S(1)}, bf16[64,1024]{1,0:T(8,128)(2,1)S(1)}, u32[]{:S(2)}, u32[]{:S(2)}) collective-permute-start(bf16[64,1024]{1,0:T(8,128)(2,1)S(1)} %collective-permute-done.10.r0), channel_id=1, source_target_pairs={{0,2},{1,3},{2,0},{3,1},{4,6},{5,7},{6,4},{7,5},{8,10},{9,11},{10,... | collective-permute-start | bytes 393224 | tf_op jit(solution)/shard_map/ppermute | solution.py:353
  279.9 8.6 %collective-permute-start.11 = (bf16[64,1024]{1,0:T(8,128)(2,1)S(1)}, bf16[64,1024]{1,0:T(8,128)(2,1)S(1)}, u32[]{:S(2)}, u32[]{:S(2)}) collective-permute-start(bf16[64,1024]{1,0:T(8,128)(2,1)S(1)} %collective-permute-done.10.r0), channel_id=1, source_target_pairs={{0,1},{1,0},{2,3},{3,2},{4,5},{5,4},{6,7},{7,6},{8,9},{9,8},{10,11... | collective-permute-start | bytes 393224 | tf_op jit(solution)/shard_map/ppermute | solution.py:353
  284.2 4.3 %copy-start.7 = (s32[8]{0:T(128)S(1)}, s32[8]{0:T(128)}, u32[]{:S(2)}) copy-start(s32[8]{0:T(128)} %count.3) | copy-start | bytes 100
  294.8 16.0 %all-to-all-start.6 = ((bf16[4,256,256]{2,1,0:T(8,128)(2,1)}), bf16[4,256,256]{2,1,0:T(8,128)(2,1)S(1)}, u32[]{:S(2)}, u32[]{:S(2)}) async-start(bf16[4,256,256]{2,1,0:T(8,128)(2,1)} %shard_map.221), calls=%async_computation.6 | async-start | bytes 1048576 | tf_op jit(solution)/shard_map/all_to_all | solution.py:321
Sparse Core Ops, SparseCore 0:
  57.5 88.1 all-gather.3
